TPU v7x, 32 devices: a whole 2x2x4 slice. The times are simulated.
32 devices in a mesh: replica: 8 (over z, core), tp: 4 (over y, x).
Axes of the slice: x: 2, y: 2, z: 4, core: 2. Of those that a mesh axis runs over, the one named last changes fastest.
Arguments:
- token_ids: int32 [128], replicated, may hold values from 0 to 8191
- embed_table: bfloat16 [8192, 8192], P('replica', 'tp'), may hold values from -6 to 6
- norm_gain: bfloat16 [8192], replicated, may hold values from 0.099609375 to 1.8984375
- w_query: bfloat16 [8192, 4096], P(('replica', 'tp')), may hold values from -0.0625 to 0.0625
- w_keyvalue: bfloat16 [8192, 2, 512], P(('replica', 'tp')), may hold values from -0.0625 to 0.0625
- key_cache: bfloat16 [512, 1024, 128], P(('replica', 'tp')), may hold values from -360 to 360
- value_cache: bfloat16 [512, 1024, 128], P(('replica', 'tp')), may hold values from -6 to 6
- cache_lengths: int32 [128], P('replica'), may hold values from 1 to 1024, as said below
Outputs:
- context: bfloat16 [512, 1024], P(('replica', 'tp'))
- query_weight_tp: bfloat16 [8192, 4096], P(None, 'tp')
- keyvalue_weight_tp: bfloat16 [8192, 2, 512], P(None, None, 'tp')
Inputs may be any that keep to these rules, and one draw needn't show every extreme that they name: `cache_lengths`: some sequence has exactly 1024 filled slots.
All inputs are finite; a program needn't handle non-finite values.
Results may differ from a plain program's by a relative error of at most 0.019.
The roundings to bfloat16 on the way count: a program that leaves them out, or rounds other values in their place, can miss the bound.
Values may be sent and summed in bfloat16 or wider, within the bound.
A program may use at most 128 MiB of HBM per device.

v0:
```python
import jax
import jax.numpy as jnp
from jax import lax
from jax.sharding import PartitionSpec as P


def attend(query, keys, values, key_new, value_new, lengths):
    scale = query.shape[-1] ** (-0.5)
    scores = jnp.einsum("rgd,rcd->rgc", query, keys, preferred_element_type=jnp.float32) * scale
    position = lax.broadcasted_iota(jnp.int32, scores.shape, 2)
    scores = jnp.where(position < lengths[:, None, None], scores, -jnp.inf)
    own = jnp.einsum("rgd,rd->rg", query, key_new, preferred_element_type=jnp.float32) * scale
    top = jnp.maximum(jnp.max(scores, axis=2), own)
    weights = jnp.exp(scores - top[:, :, None])
    own_weight = jnp.exp(own - top)
    total = jnp.sum(weights, axis=2) + own_weight
    weights = (weights / total[:, :, None]).astype(jnp.bfloat16)
    own_weight = (own_weight / total).astype(jnp.bfloat16)
    context = jnp.einsum("rgc,rcd->rgd", weights, values, preferred_element_type=jnp.float32)
    context = (
        context
        + own_weight.astype(jnp.float32)[:, :, None] * value_new.astype(jnp.float32)[:, None, :]
    )
    return context.astype(jnp.bfloat16)


def per_device(
    token_ids, embed_table, norm_gain, w_query, w_keyvalue, key_cache, value_cache, cache_lengths
):
    group_index = lax.axis_index("replica")
    tp_index = lax.axis_index("tp")
    vocab_rows, feature_cols = embed_table.shape
    batch = cache_lengths.shape[0]
    first_id = group_index * vocab_rows
    picked = token_ids - first_id
    columns = lax.broadcasted_iota(jnp.int32, (batch * lax.axis_size("replica"), vocab_rows), 1)
    onehot = (picked[:, None] == columns).astype(jnp.bfloat16)
    embedded = lax.psum_scatter(
        jnp.dot(onehot, embed_table, preferred_element_type=jnp.float32),
        "replica",
        scatter_dimension=0,
        tiled=True,
    ).astype(jnp.bfloat16)
    whole = lax.all_gather(embedded, "tp", axis=1, tiled=True)
    values32 = whole.astype(jnp.float32)
    mean_square = jnp.mean(values32 * values32, axis=1, keepdims=True)
    normed = (values32 * lax.rsqrt(mean_square + 1e-05) * norm_gain.astype(jnp.float32)).astype(
        jnp.bfloat16
    )
    width = normed.shape[1]
    query_rows = w_query.reshape(w_query.shape[0], 1, w_query.shape[1])
    query_mid, pair_mid = (
        lax.all_to_all(query_rows, "tp", split_axis=2, concat_axis=0, tiled=True),
        lax.all_to_all(w_keyvalue, "tp", split_axis=2, concat_axis=0, tiled=True),
    )
    flat_query = query_mid.reshape(query_mid.shape[0], query_mid.shape[2])
    pair_cols = pair_mid.shape[2]
    flat_pair = pair_mid.reshape(pair_mid.shape[0], 2 * pair_cols)
    query_full, pair_full = (
        lax.all_gather(flat_query, "replica", axis=0, tiled=True),
        lax.all_gather(flat_pair, "replica", axis=0, tiled=True),
    )
    query_acc = jnp.dot(normed, query_full, preferred_element_type=jnp.float32)
    pair_acc = jnp.dot(normed, pair_full, preferred_element_type=jnp.float32)
    query_local = query_acc.astype(jnp.bfloat16)
    pair_local = pair_acc.astype(jnp.bfloat16).reshape(batch, 2, pair_cols)
    query_heads, pair_heads = (
        lax.all_gather(query_local, "tp", axis=1, tiled=True),
        lax.all_gather(pair_local, "tp", axis=2, tiled=True),
    )
    head_size = key_cache.shape[2]
    kv_heads = pair_heads.shape[2] // head_size
    group = query_heads.shape[1] // (kv_heads * head_size)
    rows_here = key_cache.shape[0]
    first_row = tp_index * rows_here
    query_grouped = (
        query_heads.reshape(batch, kv_heads, group, head_size)
        .transpose(1, 0, 2, 3)
        .reshape(kv_heads * batch, group, head_size)
    )
    key_grouped = (
        pair_heads[:, 0]
        .reshape(batch, kv_heads, head_size)
        .transpose(1, 0, 2)
        .reshape(kv_heads * batch, head_size)
    )
    value_grouped = (
        pair_heads[:, 1]
        .reshape(batch, kv_heads, head_size)
        .transpose(1, 0, 2)
        .reshape(kv_heads * batch, head_size)
    )
    query_mine = lax.dynamic_slice_in_dim(query_grouped, first_row, rows_here, 0)
    key_mine = lax.dynamic_slice_in_dim(key_grouped, first_row, rows_here, 0)
    value_mine = lax.dynamic_slice_in_dim(value_grouped, first_row, rows_here, 0)
    sequence = (first_row + lax.broadcasted_iota(jnp.int32, (rows_here,), 0)) % batch
    matches = sequence[:, None] == lax.broadcasted_iota(jnp.int32, (rows_here, batch), 1)
    row_lengths = jnp.sum(jnp.where(matches, cache_lengths[None, :], 0), axis=1)
    context = attend(query_mine, key_cache, value_cache, key_mine, value_mine, row_lengths)
    context = context.reshape(rows_here, group * head_size)
    return (context, query_full, pair_full.reshape(width, 2, pair_cols))


def solution(mesh):
    return jax.shard_map(
        per_device,
        mesh=mesh,
        in_specs=(
            P(),
            P("replica", "tp"),
            P(),
            P(("replica", "tp"), None),
            P(("replica", "tp"), None, None),
            P(("replica", "tp"), None, None),
            P(("replica", "tp"), None, None),
            P("replica"),
        ),
        out_specs=(P(("replica", "tp"), None), P(None, "tp"), P(None, None, "tp")),
        check_vma=False,
    )
```

profile of v0, /device:TPU:0, one launch (start us, length us, event | category | flops | bytes accessed | tf_op | source)
XLA Modules:
  0.0 279.0 jit_solution(18418797829905342189)
XLA Ops:
  7.2 0.7 broadcast_subtract_fusion
  7.9 3.9 %fusion.6 = f32[128,2048]{1,0:T(8,128)} fusion(bf16[1024,2048]{1,0:T(8,128)(2,1)} %param.9, s32[128]{0:T(128)S(1)} %broadcast_subtract_fusion), kind=kOutput, calls=%fused_computation.17 | convolution fusion | flops 537001984 | bytes 5243392 | tf_op jit(solution)/shard_map/dot_general | solution.py:39
  11.9 1.0 copy.59
  12.9 13.5 %all_to_all.30 = bf16[256,2,512]{0,1,2:T(2,128)(2,1)S(1)} all-to-all(bf16[256,2,512]{0,1,2:T(2,128)(2,1)S(1)} %copy.59), channel_id=1, replica_groups=mesh['replica'=8,'tp'=4] {'tp'}, dimensions={2} | all-to-all | bytes 1048576 | tf_op jit(solution)/shard_map/all_to_all | solution.py:54
  27.1 0.9 copy.76
  28.1 7.1 %copy.56 = bf16[256,1,4096]{0,1,2:T(2,128)(2,1)} copy(bf16[256,1,4096]{2,0,1:T(8,128)(2,1)S(1)} %bitcast.52) | data formatting | bytes 4194304 | tf_op jit(solution)/shard_map/reshape | solution.py:51
  35.6 21.6 %reduce = bf16[4096,256]{1,0:T(8,128)(2,1)S(1)} reduce(bf16[4096,1,256]{2,1,0:T(2,128)(2,1)} %bitcast.48, bf16[]{:T(256)} %broadcast.60), dimensions={1}, to_apply=%bitcast.36.reduce_sub_computation | reduce | bytes 4194306
  57.2 2.1 reshape.81
  59.3 27.9 %all_to_all.31 = bf16[4,2,131072]{2,1,0:T(2,128)(2,1)S(1)} all-to-all(bf16[4,2,131072]{2,1,0:T(2,128)(2,1)} %reshape.81), channel_id=1, replica_groups=mesh['replica'=8,'tp'=4] {'tp'}, dimensions={0} | all-to-all | bytes 4194304 | tf_op jit(solution)/shard_map/all_to_all | solution.py:53
  87.1 3.3 %reshape.82 = bf16[4096,1,256]{2,1,0:T(2,128)(2,1)} reshape(bf16[4,2,131072]{2,1,0:T(2,128)(2,1)S(1)} %all_to_all.31) | data formatting | bytes 4194304
  90.4 2.6 copy.66
  93.0 2.4 copy.57
  95.7 0.9 convert_element_type.34
  96.6 8.4 %all_gather.15 = bf16[16,8192]{1,0:T(8,128)(2,1)S(1)} all-gather(bf16[16,2048]{1,0:T(8,128)(2,1)S(1)} %convert_element_type.34), channel_id=1, replica_groups=mesh['replica'=8,'tp'=4] {'tp'}, dimensions={1}, use_global_device_ids=true | all-gather | bytes 327680 | tf_op jit(solution)/shard_map/all_gather | solution.py:44
  105.2 3.8 %fusion.2 = bf16[2,2,8,128]{3,2,1,0:T(8,128)(2,1)S(1)} fusion(bf16[8192,256]{1,0:T(8,128)(2,1)} %all-gather.5.cloned.1.call-done, bf16[16,8192]{1,0:T(8,128)(2,1)S(1)} %all_gather.15, f32[8192]{0:T(1024)S(1)} %convert_element_type.36, f32[16]{0:T(128)S(1)} %add_rsqrt_fusion), kind=kOutput, calls=%fused_computation.6 | convolution fusion | flops 67637248 | bytes 4497472 | tf_op jit(solution)/shard_map/dot_general | solution.py:64
  109.0 7.4 %all_gather.19 = bf16[16,2,512]{2,0,1:T(8,128)(2,1)S(1)} all-gather(bf16[16,2,128]{2,0,1:T(8,128)(2,1)S(1)} %bitcast.65), channel_id=1, replica_groups=mesh['replica'=8,'tp'=4] {'tp'}, dimensions={2}, use_global_device_ids=true | all-gather | bytes 40960 | tf_op jit(solution)/shard_map/all_gather | solution.py:69
  116.5 7.0 %reshape.78 = bf16[8192,2,128]{2,1,0:T(2,128)(2,1)} reshape(bf16[8192,256]{1,0:T(8,128)(2,1)} %all-gather.5.cloned.1.call-done) | data formatting | bytes 8388608 | tf_op jit(solution)/shard_map/reshape | solution.py:101
  123.5 122.8 %all-gather.3.cloned.1.call-done = bf16[8192,1024]{1,0:T(8,128)(2,1)} async-done(((bf16[1024,1024]{1,0:T(8,128)(2,1)}), bf16[8192,1024]{1,0:T(8,128)(2,1)}) %all-gather.3.cloned.1.call-update) | async-done | bytes 16777232 | tf_op jit(solution)/shard_map/all_gather | solution.py:60
  246.3 8.2 %convolution_convert_fusion = bf16[16,1024]{1,0:T(8,128)(2,1)S(1)} fusion(bf16[8192,1024]{1,0:T(8,128)(2,1)} %all-gather.3.cloned.1.call-done, bf16[16,8192]{1,0:T(8,128)(2,1)S(1)} %all_gather.15, f32[8192]{0:T(1024)S(1)} %convert_element_type.36, f32[16]{0:T(128)S(1)} %add_rsqrt_fusion), kind=kOutput, calls=%fused_computation.4 | convolution fusion | flops 268976128 | bytes 17104960 | tf_op jit(solution)/shard_map/dot_general | solution.py:63
  254.5 8.7 %all_gather.17 = bf16[16,4096]{1,0:T(8,128)(2,1)S(1)} all-gather(bf16[16,1024]{1,0:T(8,128)(2,1)S(1)} %convolution_convert_fusion), channel_id=1, replica_groups=mesh['replica'=8,'tp'=4] {'tp'}, dimensions={1}, use_global_device_ids=true | all-gather | bytes 163840 | tf_op jit(solution)/shard_map/all_gather | solution.py:68
  263.4 1.3 fusion.23
  265.0 0.7 fusion.1
  265.7 0.6 copy.77
  266.3 6.2 %copy.80 = bf16[8192,1024]{1,0:T(8,128)(2,1)} copy(bf16[8192,1024]{1,0:T(8,128)(2,1)S(1)} %bitcast.47) | data formatting | bytes 33554432
  (50 shorter events, 2.2 us)
Async XLA Ops:
  7.2 4.8 %copy-start.3 = (bf16[256,2,512]{2,1,0:T(2,128)(2,1)S(1)}, bf16[256,2,512]{2,1,0:T(2,128)(2,1)}, u32[]{:S(2)}) copy-start(bf16[256,2,512]{2,1,0:T(2,128)(2,1)} %param.12) | copy-start | bytes 1572868
  7.2 88.5 %reduce-scatter.2.cloned.1.call-start = ((), (), s32[]{:S(2)}) async-start(), calls=%async_computation.3 | async-start | bytes 1179648 | tf_op jit(solution)/shard_map/reduce_scatter | solution.py:38
  11.8 16.2 %copy-start.2 = (bf16[256,4096]{1,0:T(8,128)(2,1)S(1)}, bf16[256,4096]{1,0:T(8,128)(2,1)}, u32[]{:S(2)}) copy-start(bf16[256,4096]{1,0:T(8,128)(2,1)} %param.11) | copy-start | bytes 6291460
  11.9 93.3 %all-gather.5.cloned.1.call-start = ((), (), s32[]{:S(2)}) async-start(), calls=%async_computation.5 | async-start | bytes 4718592 | tf_op jit(solution)/shard_map/all_gather | solution.py:61
  28.0 218.3 %all-gather.3.cloned.1.call-start = ((), (), s32[]{:S(2)}) async-start(), calls=%async_computation.4 | async-start | bytes 18874368 | tf_op jit(solution)/shard_map/all_gather | solution.py:60
  93.0 2.4 copy-start.4
  93.0 2.5 copy-start.5
  246.3 17.1 %copy-start.1 = (bf16[16,1024,128]{2,1,0:T(8,128)(2,1)S(1)}, bf16[16,1024,128]{2,1,0:T(8,128)(2,1)}, u32[]{:S(2)}) copy-start(bf16[16,1024,128]{2,1,0:T(8,128)(2,1)} %param.13) | copy-start | bytes 12582916
  246.3 20.0 %slice-start = ((s8[16777216]{0:T(1024)(128)(4,1)}), s8[4194304]{0:T(1024)(128)(4,1)S(1)}, s32[]{:S(2)}) async-start(s8[16777216]{0:T(1024)(128)(4,1)} %bitcast.46), calls=%async_computation.6 | async-start | bytes 8388608
  246.3 20.0 %slice-start.1 = ((s8[16777216]{0:T(1024)(128)(4,1)}), s8[4194304]{0:T(1024)(128)(4,1)S(1)}, s32[]{:S(2)}) async-start(s8[16777216]{0:T(1024)(128)(4,1)} %bitcast.46), calls=%async_computation.7 | async-start | bytes 8388608
  246.3 20.0 %slice-start.2 = ((s8[16777216]{0:T(1024)(128)(4,1)}), s8[4194304]{0:T(1024)(128)(4,1)S(1)}, s32[]{:S(2)}) async-start(s8[16777216]{0:T(1024)(128)(4,1)} %bitcast.46), calls=%async_computation.8 | async-start | bytes 8388608
  254.5 10.4 %copy-start = (bf16[16,1024,128]{2,1,0:T(8,128)(2,1)S(1)}, bf16[16,1024,128]{2,1,0:T(8,128)(2,1)}, u32[]{:S(2)}) copy-start(bf16[16,1024,128]{2,1,0:T(8,128)(2,1)} %param.14) | copy-start | bytes 12582916
  263.4 2.9 %slice-start.3 = ((s8[16777216]{0:T(1024)(128)(4,1)}), s8[4194304]{0:T(1024)(128)(4,1)S(1)}, s32[]{:S(2)}) async-start(s8[16777216]{0:T(1024)(128)(4,1)} %bitcast.46), calls=%async_computation.9 | async-start | bytes 8388608
Sparse Core Ops, SparseCore 0:
  12.0 35.2 reduce-scatter.1
  48.9 45.1 all-gather.4
  96.4 149.8 all-gather.2
where the time goes:
time: 280 us; the launch traced here: 279 us
  waiting for transfers between devices  123 us (44%)
  blocking collectives  65.9 us (24%)
  local copies, waits for them, and re-layouts  34.3 us (12%)
  other arithmetic  23.9 us (9%)
  matrix products  18 us (6%)
  between operations  14 us (5%)
    all_gather x1, waiting for transfers between devices, per_device(): lax.all_gather(flat_query, 'replica', axis=0, tiled=True)  123 us
    all_to_all x1, blocking collectives, per_device(): lax.all_to_all(query_rows, 'tp', split_axis=2, concat_axis=0, tiled=True)  27.9 us
    unnamed x2, other arithmetic  21.6 us
    unnamed x29, local copies, waits for them, and re-layouts  17.2 us
    all_to_all x1, blocking collectives, per_device(): lax.all_to_all(w_keyvalue, 'tp', split_axis=2, concat_axis=0, tiled=True)  13.5 us
    all_gather x1, blocking collectives, per_device(): lax.all_gather(query_local, 'tp', axis=1, tiled=True)  8.68 us
    all_gather x1, blocking collectives, per_device(): whole = lax.all_gather(embedded, 'tp', axis=1, tiled=True)  8.37 us
    dot_general x1, matrix products, per_device(): query_acc = jnp.dot(normed, query_full, preferred_element_type=jnp.float32)  8.22 us
  transfers between devices with their start and end apart: 3, of which 1 were waited for; matrix products, arithmetic and copies ran while one was open for 19% of the time, Pallas kernels for 0%

commit v1 on v0

--- a/solution.py
+++ b/solution.py
@@ -2,6 +2,16 @@
 import jax.numpy as jnp
 from jax import lax
 from jax.sharding import PartitionSpec as P
+
+view_yards = lambda xin, ndim_at: jnp.concatenate(
+    lax.all_to_all(
+        jnp.stack([xin for _ in range(lax.psum(1, "replica"))]),
+        split_axis=0,
+        concat_axis=0,
+        axis_name="replica",
+    ),
+    axis=ndim_at,
+)
 
 
 def attend(query, keys, values, key_new, value_new, lengths):
@@ -57,7 +67,7 @@
     pair_cols = pair_mid.shape[2]
     flat_pair = pair_mid.reshape(pair_mid.shape[0], 2 * pair_cols)
     query_full, pair_full = (
-        lax.all_gather(flat_query, "replica", axis=0, tiled=True),
+        view_yards(flat_query, 0),
         lax.all_gather(flat_pair, "replica", axis=0, tiled=True),
     )
     query_acc = jnp.dot(normed, query_full, preferred_element_type=jnp.float32)

time: 280 us -> 547 us (1.95)
  waiting for transfers between devices: 123 us -> 396 us
  blocking collectives: 65.9 us -> 26.8 us
  local copies, waits for them, and re-layouts: 34.3 us -> 53.9 us
  starting transfers between devices: 0.12 us -> 14.6 us
    all_to_all x0 -> x3, waiting for transfers between devices: none -> 243 us  [the longest x1 220 us: lax.all_to_all(jnp.stack([xin for _ in range(lax.psum(1, 'replica'))]), s...]
    all_gather x1 -> x0, waiting for transfers between devices: 123 us -> none  [per_device(): lax.all_gather(flat_query, 'replica', axis=0, tiled=True)]
    all_gather x1, waiting for transfers between devices: 0.02 us -> 82.5 us  [per_device(): lax.all_gather(flat_pair, 'replica', axis=0, tiled=True)]
    reduce_scatter x1, waiting for transfers between devices: 0.01 us -> 69.7 us  [per_device(): lax.psum_scatter(jnp.dot(onehot, embed_table, preferred_element_type=jnp....]
    all_to_all x2 -> x0, blocking collectives: 41.4 us -> none  [the longest x1 27.9 us: per_device(): lax.all_to_all(query_rows, 'tp', split_axis=2, concat_axis=0, tiled=True)]
    all_to_all x0 -> x3, starting transfers between devices: none -> 14.5 us  [the longest x1 5.87 us: lax.all_to_all(jnp.stack([xin for _ in range(lax.psum(1, 'replica'))]), s...]
    unnamed x29 -> x21, local copies, waits for them, and re-layouts: 17.2 us -> 27.2 us
    another operation x0 -> x1, local copies, waits for them, and re-layouts: none -> 6.16 us  [jnp.stack([xin for _ in range(lax.psum(1, 'replica'))])]
  transfers between devices with their start and end apart: 3 -> 5, of which waited for: 1 -> 4; matrix products, arithmetic and copies ran while one was open for 19% -> 5% of each run, Pallas kernels for 0% -> 0%
where the time goes in v1:
time: 547 us; the launch traced here: 545 us
  waiting for transfers between devices  396 us (72%)
  local copies, waits for them, and re-layouts  53.9 us (10%)
  blocking collectives  26.8 us (5%)
  other arithmetic  23.2 us (4%)
  matrix products  17.2 us (3%)
  starting transfers between devices  14.6 us (3%)
  between operations  14.2 us (3%)
    all_to_all x1, waiting for transfers between devices, lax.all_to_all(jnp.stack([xin for _ in range(lax.psum(1, 'replica'))]), s...  220 us
    all_gather x1, waiting for transfers between devices, per_device(): lax.all_gather(flat_pair, 'replica', axis=0, tiled=True)  82.5 us
    reduce_scatter x1, waiting for transfers between devices, per_device(): lax.psum_scatter(jnp.dot(onehot, embed_table, preferred_element_type=jnp....  69.7 us
    unnamed x21, local copies, waits for them, and re-layouts  27.2 us
    all_to_all x1, waiting for transfers between devices, per_device(): lax.all_to_all(query_rows, 'tp', split_axis=2, concat_axis=0, tiled=True)  22.9 us
    unnamed x1, other arithmetic  21.6 us
  transfers between devices with their start and end apart: 5, of which 4 were waited for; matrix products, arithmetic and copies ran while one was open for 5% of the time, Pallas kernels for 0%

profile of v1, /device:TPU:0, one launch (start us, length us, event | category | flops | bytes accessed | tf_op | source)
XLA Modules:
  0.0 545.4 jit_solution(15128236289440982073)
XLA Ops:
  7.2 10.0 %copy.48 = bf16[256,1,4096]{0,1,2:T(2,128)(2,1)} copy(bf16[256,1,4096]{2,0,1:T(8,128)(2,1)} %bitcast.51) | data formatting | bytes 4194304 | tf_op jit(solution)/shard_map/reshape | solution.py:61
  17.6 21.6 %reduce = bf16[4096,256]{1,0:T(8,128)(2,1)S(1)} reduce(bf16[4096,1,256]{2,1,0:T(2,128)(2,1)} %bitcast.47, bf16[]{:T(256)} %broadcast.61), dimensions={1}, to_apply=%bitcast.37.reduce_sub_computation | reduce | bytes 4194306
  39.2 2.1 reshape.83
  41.3 5.2 all-to-all-start
  46.5 2.0 copy.51
  48.5 22.9 %all-to-all-done = bf16[4,2,131072]{2,1,0:T(2,128)(2,1)S(1)} async-done(((bf16[4,2,131072]{2,1,0:T(2,128)(2,1)}), bf16[4,2,131072]{2,1,0:T(2,128)(2,1)S(1)}, u32[]{:S(2)}, u32[]{:S(2)}) %all-to-all-start) | async-done | bytes 2097184 | tf_op jit(solution)/shard_map/all_to_all | solution.py:63
  71.4 3.5 all-to-all-start.2
  74.8 3.3 reshape.84
  78.1 3.9 copy.58
  82.0 3.0 copy.49
  85.0 6.2 %stack.3 = bf16[8,1024,1024]{2,1,0:T(8,128)(2,1)} broadcast(bf16[1024,1024]{1,0:T(8,128)(2,1)S(1)} %bitcast.49), dimensions={1,2} | broadcast | bytes 18874368 | tf_op jit(solution)/shard_map/stack | solution.py:8
  91.2 5.9 %all-to-all-start.1 = ((bf16[8,1024,1024]{2,1,0:T(8,128)(2,1)}), bf16[8,1024,1024]{2,1,0:T(8,128)(2,1)}, u32[]{:S(2)}, u32[]{:S(2)}) async-start(bf16[8,1024,1024]{2,1,0:T(8,128)(2,1)} %stack.3), calls=%async_computation.2 | async-start | bytes 33554432 | tf_op jit(solution)/shard_map/all_to_all | solution.py:7
  97.1 3.9 fusion.6
  102.9 69.7 %reduce-scatter.2.cloned.1.call-done = f32[16,2048]{1,0:T(8,128)} async-done(((f32[128,2048]{1,0:T(8,128)}), f32[16,2048]{1,0:T(8,128)}) %reduce-scatter.2.cloned.1.call-update) | async-done | bytes 131088 | tf_op jit(solution)/shard_map/reduce_scatter | solution.py:48
  173.5 9.4 %all_gather.12 = bf16[16,8192]{1,0:T(8,128)(2,1)S(1)} all-gather(bf16[16,2048]{1,0:T(8,128)(2,1)S(1)} %convert_element_type.34), channel_id=1, replica_groups=mesh['replica'=8,'tp'=4] {'tp'}, dimensions={1}, use_global_device_ids=true | all-gather | bytes 327680 | tf_op jit(solution)/shard_map/all_gather | solution.py:54
  183.1 82.5 %all-gather.2.cloned.1.call-done = bf16[8192,256]{1,0:T(8,128)(2,1)} async-done(((bf16[1024,256]{1,0:T(8,128)(2,1)}), bf16[8192,256]{1,0:T(8,128)(2,1)}) %all-gather.2.cloned.1.call-update) | async-done | bytes 4194320 | tf_op jit(solution)/shard_map/all_gather | solution.py:71
  265.6 2.9 fusion.2
  268.5 8.2 %all_gather.15 = bf16[16,2,512]{2,0,1:T(8,128)(2,1)S(1)} all-gather(bf16[16,2,128]{2,0,1:T(8,128)(2,1)S(1)} %bitcast.64), channel_id=1, replica_groups=mesh['replica'=8,'tp'=4] {'tp'}, dimensions={2}, use_global_device_ids=true | all-gather | bytes 40960 | tf_op jit(solution)/shard_map/all_gather | solution.py:79
  276.8 6.9 %reshape.80 = bf16[8192,2,128]{2,1,0:T(2,128)(2,1)} reshape(bf16[8192,256]{1,0:T(8,128)(2,1)} %all-gather.2.cloned.1.call-done) | data formatting | bytes 8388608 | tf_op jit(solution)/shard_map/reshape | solution.py:111
  283.7 220.5 %all-to-all-done.1 = bf16[8,1024,1024]{2,1,0:T(8,128)(2,1)} async-done(((bf16[8,1024,1024]{2,1,0:T(8,128)(2,1)}), bf16[8,1024,1024]{2,1,0:T(8,128)(2,1)}, u32[]{:S(2)}, u32[]{:S(2)}) %all-to-all-start.1) | async-done | bytes 16777248 | tf_op jit(solution)/shard_map/all_to_all | solution.py:7
  504.2 8.2 %convolution_convert_fusion = bf16[16,1024]{1,0:T(8,128)(2,1)S(1)} fusion(bf16[8192,1024]{1,0:T(8,128)(2,1)} %bitcast.3, bf16[16,8192]{1,0:T(8,128)(2,1)S(1)} %all_gather.12, f32[8192]{0:T(1024)S(1)} %convert_element_type.36, f32[16]{0:T(128)S(1)} %add_rsqrt_fusion), kind=kOutput, calls=%fused_computation.4 | convolution fusion | flops 268976128 | bytes 17104960 | tf_op jit(solution)/shard_map/dot_general | solution.py:73
  512.4 9.2 %all_gather.13 = bf16[16,4096]{1,0:T(8,128)(2,1)S(1)} all-gather(bf16[16,1024]{1,0:T(8,128)(2,1)S(1)} %convolution_convert_fusion), channel_id=1, replica_groups=mesh['replica'=8,'tp'=4] {'tp'}, dimensions={1}, use_global_device_ids=true | all-gather | bytes 163840 | tf_op jit(solution)/shard_map/all_gather | solution.py:78
  521.8 1.3 fusion.23
  524.7 13.9 %copy.72 = bf16[8192,1024]{1,0:T(8,128)(2,1)} copy(bf16[8192,1024]{1,0:T(8,128)(2,1)} %bitcast.3) | data formatting | bytes 33554432
  (43 shorter events, 5.3 us)
Async XLA Ops:
  39.2 7.3 %copy-start.2 = (bf16[256,2,512]{2,1,0:T(2,128)(2,1)S(1)}, bf16[256,2,512]{2,1,0:T(2,128)(2,1)}, u32[]{:S(2)}) copy-start(bf16[256,2,512]{2,1,0:T(2,128)(2,1)} %param.12) | copy-start | bytes 1572868
  41.3 30.1 %all-to-all-start = ((bf16[4,2,131072]{2,1,0:T(2,128)(2,1)}), bf16[4,2,131072]{2,1,0:T(2,128)(2,1)S(1)}, u32[]{:S(2)}, u32[]{:S(2)}) async-start(bf16[4,2,131072]{2,1,0:T(2,128)(2,1)} %reshape.83), calls=%async_computation.1 | async-start | bytes 4194304 | tf_op jit(solution)/shard_map/all_to_all | solution.py:63
  71.4 13.6 %all-to-all-start.2 = ((bf16[256,2,512]{0,1,2:T(2,128)(2,1)}), bf16[256,2,512]{0,1,2:T(2,128)(2,1)S(1)}, u32[]{:S(2)}, u32[]{:S(2)}) async-start(bf16[256,2,512]{0,1,2:T(2,128)(2,1)} %copy.51), calls=%async_computation.3 | async-start | bytes 1048576 | tf_op jit(solution)/shard_map/all_to_all | solution.py:64
  91.2 5.9 %copy-start.4 = (s32[128]{0:T(128)S(1)}, s32[128]{0:T(128)}, u32[]{:S(2)}) copy-start(s32[128]{0:T(128)} %param.8) | copy-start | bytes 1540
  91.2 413.0 %all-to-all-start.1 = ((bf16[8,1024,1024]{2,1,0:T(8,128)(2,1)}), bf16[8,1024,1024]{2,1,0:T(8,128)(2,1)}, u32[]{:S(2)}, u32[]{:S(2)}) async-start(bf16[8,1024,1024]{2,1,0:T(8,128)(2,1)} %stack.3), calls=%async_computation.2 | async-start | bytes 33554432 | tf_op jit(solution)/shard_map/all_to_all | solution.py:7
  97.0 75.5 %reduce-scatter.2.cloned.1.call-start = ((), (), s32[]{:S(2)}) async-start(), calls=%async_computation.4 | async-start | bytes 1179648 | tf_op jit(solution)/shard_map/reduce_scatter | solution.py:48
  97.1 5.6 %copy-start.3 = (bf16[8192]{0:T(1024)(128)(2,1)S(1)}, bf16[8192]{0:T(1024)(128)(2,1)}, u32[]{:S(2)}) copy-start(bf16[8192]{0:T(1024)(128)(2,1)} %param.10) | copy-start | bytes 49156
  97.1 5.6 %copy-start.5 = (s32[16]{0:T(128)S(1)}, s32[16]{0:T(128)}, u32[]{:S(2)}) copy-start(s32[16]{0:T(128)} %param.15) | copy-start | bytes 196
  101.1 164.5 %all-gather.2.cloned.1.call-start = ((), (), s32[]{:S(2)}) async-start(), calls=%async_computation.5 | async-start | bytes 4718592 | tf_op jit(solution)/shard_map/all_gather | solution.py:71
  504.2 17.6 %copy-start.1 = (bf16[16,1024,128]{2,1,0:T(8,128)(2,1)S(1)}, bf16[16,1024,128]{2,1,0:T(8,128)(2,1)}, u32[]{:S(2)}) copy-start(bf16[16,1024,128]{2,1,0:T(8,128)(2,1)} %param.13) | copy-start | bytes 12582916
  512.4 10.9 %copy-start = (bf16[16,1024,128]{2,1,0:T(8,128)(2,1)S(1)}, bf16[16,1024,128]{2,1,0:T(8,128)(2,1)}, u32[]{:S(2)}) copy-start(bf16[16,1024,128]{2,1,0:T(8,128)(2,1)} %param.14) | copy-start | bytes 12582916
Sparse Core Ops, SparseCore 0:
  101.2 71.3 reduce-scatter.1
  174.2 91.3 all-gather.1
